TPU v7x, 32 devices: a whole 2x2x4 slice. The times are simulated.
32 devices in a mesh: seq: 8 (over y, x, core), head: 4 (over z).
Axes of the slice: x: 2, y: 2, z: 4, core: 2. Of those that a mesh axis runs over, the one named last changes fastest.
Arguments:
- queries: bfloat16 [1024, 1024], P('seq', 'head'), may hold values from -24 to 24
- keys_values: bfloat16 [2, 1024, 128], P(None, 'seq'), may hold values from -6 to 6
- out_weight: bfloat16 [2560, 8, 128], P('head'), may hold values from -0.125 to 0.125
- out_grad: bfloat16 [1024, 2560], P('seq'), may hold values from -6 to 6
- positions: int32 [1024], replicated, may hold values from 0 to 1023, as said below
Outputs:
- d_query: bfloat16 [1024, 1024], P('seq', 'head')
- d_out_weight: float32 [2560, 8, 128], P('seq', 'head')
Inputs may be any that keep to these rules, and one draw needn't show every extreme that they name: positions holds each of 0 to 1023 once, in runs of 64 consecutive rows with consecutive positions, each run starting at a row and a position that are multiples of 64.
All inputs are finite; a program needn't handle non-finite values.
Results may differ from a plain program's by a relative error of at most 0.007.
Values may be sent and summed in bfloat16 or wider, within the bound.
No kernel may reach another device: no remote copies, remote signals or barrier semaphores. Data moves between devices by JAX's collectives and lax.ppermute only.
A program may use at most 64 MiB of HBM per device.

v0:
```python
import math
import jax
import jax.numpy as jnp
from jax import lax
from jax.sharding import PartitionSpec as P

HD = 128
GROUP = 8
big_negative = -1e30


def attend_block(query_rows, query_pos, block_kv, key_pos, scale):
    scores = (
        lax.dot_general(
            query_rows, block_kv[0], (((1,), (1,)), ((), ())), preferred_element_type=jnp.float32
        )
        * scale
    )
    visible = key_pos[None, :] <= query_pos[:, None]
    return (jnp.where(visible, scores, big_negative), visible)


def sweep(step_fn, states, key_piece, offset, positions):
    span_size = key_piece.shape[1]
    block_size = math.gcd(span_size, 1024)

    def step(step_index, inner):
        block_kv = lax.dynamic_slice_in_dim(key_piece, step_index * block_size, block_size, 1)
        key_pos = lax.dynamic_slice_in_dim(
            positions, offset + step_index * block_size, block_size, 0
        )
        return step_fn(inner, block_kv, key_pos)

    return lax.fori_loop(0, span_size // block_size, step, states)


def body(queries, keys_values, out_weight, out_grad, positions):
    token_count = queries.shape[0]
    head_count = queries.shape[1] // HD
    scale = HD ** (-0.5)
    seq_index = lax.axis_index("seq")
    head_index = lax.axis_index("head")
    kv_group = head_index * head_count // GROUP
    own_kv = lax.dynamic_slice_in_dim(keys_values, kv_group * HD, HD, 2)
    own_pos = lax.dynamic_slice_in_dim(positions, seq_index * token_count, token_count, 0)
    query_pos = jnp.repeat(own_pos, head_count)
    query_rows = queries.reshape(token_count * head_count, HD)
    d_attn = jnp.einsum(
        "td,dhc->thc",
        out_grad,
        lax.all_to_all(out_weight, "head", split_axis=1, concat_axis=0, tiled=True),
        preferred_element_type=jnp.float32,
    )
    d_attn = d_attn.astype(jnp.bfloat16).reshape(token_count * head_count, HD)
    row_total = token_count * head_count
    zeros_col = jnp.zeros((row_total, 1), jnp.float32)
    zeros_rows = jnp.zeros((row_total, HD), jnp.float32)
    lowest_col = jnp.full((row_total, 1), big_negative, jnp.float32)
    all_kv = lax.all_gather(own_kv, "seq", axis=1, tiled=True)

    def run_sweep(step_fn, init):
        return sweep(step_fn, init, all_kv, 0, positions)

    def stats_step(states, block_kv, key_pos):
        top, norm = states
        scores, visible = attend_block(query_rows, query_pos, block_kv, key_pos, scale)
        new_top = jnp.maximum(top, jnp.max(scores, axis=1, keepdims=True))
        weights = jnp.where(visible, jnp.exp(scores - new_top), 0.0)
        norm = jnp.exp(top - new_top) * norm + jnp.sum(weights, axis=1, keepdims=True)
        return (new_top, norm)

    top, norm = run_sweep(stats_step, (lowest_col, zeros_col))

    def block_probs(block_kv, key_pos):
        scores, visible = attend_block(query_rows, query_pos, block_kv, key_pos, scale)
        return jnp.where(visible, jnp.exp(scores - top), 0.0) / norm

    def out_step(acc_out, block_kv, key_pos):
        probs = block_probs(block_kv, key_pos)
        return acc_out + jnp.dot(
            probs.astype(jnp.bfloat16), block_kv[1], preferred_element_type=jnp.float32
        )

    attn_full = run_sweep(out_step, zeros_rows)
    delta = jnp.sum(d_attn.astype(jnp.float32) * attn_full, axis=1, keepdims=True)

    def grad_step(acc_grad, block_kv, key_pos):
        probs = block_probs(block_kv, key_pos)
        dprob = lax.dot_general(
            d_attn, block_kv[1], (((1,), (1,)), ((), ())), preferred_element_type=jnp.float32
        )
        dscore = (probs * (dprob - delta)).astype(jnp.bfloat16)
        return acc_grad + jnp.dot(dscore, block_kv[0], preferred_element_type=jnp.float32)

    d_rows = run_sweep(grad_step, zeros_rows) * scale
    attn = attn_full.astype(jnp.bfloat16).reshape(token_count, head_count, HD)
    d_query = d_rows.astype(jnp.bfloat16).reshape(token_count, head_count * HD)
    d_out_weight = lax.psum_scatter(
        jnp.einsum("td,thc->dhc", out_grad, attn, preferred_element_type=jnp.float32),
        "seq",
        scatter_dimension=0,
        tiled=True,
    )
    return (d_query, d_out_weight)


def solution(mesh):
    return jax.shard_map(
        body,
        mesh=mesh,
        in_specs=(
            P("seq", "head"),
            P(None, "seq", None),
            P("head", None, None),
            P("seq", None),
            P(),
        ),
        out_specs=(P("seq", "head"), P("seq", "head", None)),
        check_vma=False,
    )
```

profile of v0, /device:TPU:0, one launch (start us, length us, event | category | flops | bytes accessed | tf_op | source)
XLA Modules:
  0.0 125.0 jit_solution(11164809730574350599)
XLA Ops:
  7.2 2.6 %copy.14 = bf16[640,8,128]{2,0,1:T(8,128)(2,1)} copy(bf16[640,8,128]{2,1,0:T(8,128)(2,1)} %param.7) | data formatting | bytes 2621440 | tf_op args[2]
  9.8 6.5 %all-to-all-start = ((bf16[640,8,128]{2,0,1:T(8,128)(2,1)}), bf16[640,8,128]{2,0,1:T(8,128)(2,1)S(1)}, u32[]{:S(2)}, u32[]{:S(2)}) async-start(bf16[640,8,128]{2,0,1:T(8,128)(2,1)} %copy.14), calls=%async_computation | async-start | bytes 2621440 | tf_op jit(solution)/shard_map/all_to_all | solution.py:51
  16.3 0.1 dynamic_slice.16
  16.4 0.1 broadcast_in_dim.38
  16.5 0.1 le.51
  16.7 9.9 %all_gather.3 = bf16[2,1024,128]{2,1,0:T(8,128)(2,1)S(1)} all-gather(bf16[2,128,128]{2,1,0:T(8,128)(2,1)S(1)} %copy-done.7), channel_id=1, replica_groups=mesh['seq'=8,'head'=4] {'seq'}, dimensions={1}, use_global_device_ids=true | all-gather | bytes 589824 | tf_op jit(solution)/shard_map/all_gather | solution.py:59
  26.5 0.4 fusion.15
  26.9 0.4 fusion.7
  27.3 0.3 fusion.6
  27.6 20.0 %all-to-all-done = bf16[640,8,128]{2,0,1:T(8,128)(2,1)S(1)} async-done(((bf16[640,8,128]{2,0,1:T(8,128)(2,1)}), bf16[640,8,128]{2,0,1:T(8,128)(2,1)S(1)}, u32[]{:S(2)}, u32[]{:S(2)}) %all-to-all-start) | async-done | bytes 1310752 | tf_op jit(solution)/shard_map/all_to_all | solution.py:51
  47.6 0.1 copy.15
  47.7 0.4 convolution_convert_fusion
  48.1 0.1 copy.16
  48.2 0.4 fusion.14
  48.6 0.2 copy-done.5
  48.8 0.5 convolution_bitcast_fusion
  49.3 3.1 %copy.18 = f32[2560,2,128]{2,1,0:T(2,128)} copy(f32[2560,2,128]{0,2,1:T(8,128)S(1)} %convolution_bitcast_fusion) | data formatting | bytes 5242880 | tf_op jit(solution)/shard_map/td,thc->dhc/dot_general | solution.py:99
  52.5 0.0 all-reduce.3.cloned.1.call-update
  52.5 0.6 copy-done.10
  53.1 0.6 dynamic-slice
  54.4 0.4 fusion.5
  54.8 0.7 reshape.37
  55.5 60.9 %all-reduce.3.cloned.1.call-done = f32[2560,2,128]{2,1,0:T(2,128)} async-done(((f32[2560,2,128]{2,1,0:T(2,128)}), f32[2560,2,128]{2,1,0:T(2,128)}) %all-reduce.3.cloned.1.call-update) | async-done | bytes 2621456
  116.4 1.7 %constant_dynamic-slice_fusion = f32[320,2,128]{2,1,0:T(2,128)} fusion(f32[2560,2,128]{2,1,0:T(2,128)} %all-reduce.3.cloned.1.call-done, u32[]{:T(128)S(6)} %multiply.1), kind=kLoop, calls=%fused_computation.23 | loop fusion | bytes 655364
  (24 shorter events, 0.1 us)
Async XLA Ops:
  7.2 40.6 %copy-start = (bf16[128,2560]{1,0:T(8,128)(2,1)S(1)}, bf16[128,2560]{1,0:T(8,128)(2,1)}, u32[]{:S(2)}) copy-start(bf16[128,2560]{1,0:T(8,128)(2,1)} %param.8) | copy-start | bytes 1966084
  9.8 6.5 %copy-start.8 = (bf16[128,256]{1,0:T(8,128)(2,1)S(1)}, bf16[128,256]{1,0:T(8,128)(2,1)}, u32[]{:S(2)}) copy-start(bf16[128,256]{1,0:T(8,128)(2,1)} %param.5) | copy-start | bytes 196612
  9.8 6.5 %copy-start.9 = (s32[1024]{0:T(1024)S(1)}, s32[1024]{0:T(1024)}, u32[]{:S(2)}) copy-start(s32[1024]{0:T(1024)} %param.9) | copy-start | bytes 12292
  9.8 6.8 %copy-start.7 = (bf16[2,128,128]{2,1,0:T(8,128)(2,1)S(1)}, bf16[2,128,128]{2,1,0:T(8,128)(2,1)}, u32[]{:S(2)}) copy-start(bf16[2,128,128]{2,1,0:T(8,128)(2,1)} %param.6) | copy-start | bytes 196612
  9.8 37.8 %all-to-all-start = ((bf16[640,8,128]{2,0,1:T(8,128)(2,1)}), bf16[640,8,128]{2,0,1:T(8,128)(2,1)S(1)}, u32[]{:S(2)}, u32[]{:S(2)}) async-start(bf16[640,8,128]{2,0,1:T(8,128)(2,1)} %copy.14), calls=%async_computation | async-start | bytes 2621440 | tf_op jit(solution)/shard_map/all_to_all | solution.py:51
  16.3 100.1 %all-reduce.3.cloned.1.call-start = ((), (), s32[]{:S(2)}) async-start(), calls=%async_computation.1 | async-start | bytes 5242880
  26.5 21.7 %copy-start.3 = (bf16[2,1024,128]{2,1,0:T(8,128)(2,1)}, bf16[2,1024,128]{2,1,0:T(8,128)(2,1)S(1)}, u32[]{:S(2)}) copy-start(bf16[2,1024,128]{2,1,0:T(8,128)(2,1)S(1)} %all_gather.3) | copy-start | bytes 1572868
  27.6 20.6 %copy-start.1 = (f32[256,1024]{1,0:T(8,128)}, f32[256,1024]{1,0:T(8,128)S(1)}, u32[]{:S(2)}) copy-start(f32[256,1024]{1,0:T(8,128)S(1)} %fusion.6) | copy-start | bytes 3145732
  48.2 0.6 copy-start.5
  52.5 0.7 copy-start.10
  52.5 1.9 %copy-start.2 = (f32[256,1024]{1,0:T(8,128)S(1)}, f32[256,1024]{1,0:T(8,128)}, u32[]{:S(2)}) copy-start(f32[256,1024]{1,0:T(8,128)} %copy-done.1) | copy-start | bytes 3145732
  52.5 1.9 %copy-start.4 = (bf16[2,1024,128]{2,1,0:T(8,128)(2,1)S(1)}, bf16[2,1024,128]{2,1,0:T(8,128)(2,1)}, u32[]{:S(2)}) copy-start(bf16[2,1024,128]{2,1,0:T(8,128)(2,1)} %copy-done.3) | copy-start | bytes 1572868
  52.5 1.9 %copy-start.6 = (bf16[128,2,128]{2,1,0:T(2,128)(2,1)S(1)}, bf16[128,2,128]{2,1,0:T(2,128)(2,1)}, u32[]{:S(2)}) copy-start(bf16[128,2,128]{2,1,0:T(2,128)(2,1)} %copy-done.5) | copy-start | bytes 196612
Sparse Core Ops, SparseCore 0:
  52.6 63.7 all-reduce.2
where the time goes:
time: 125 us
  waiting for transfers between devices  80.9 us (65%)
  between operations  14.8 us (12%)
  local copies, waits for them, and re-layouts  10.1 us (8%)
  blocking collectives  9.86 us (8%)
  starting transfers between devices  6.48 us (5%)
  matrix products  2.08 us (2%)
    unnamed x2, waiting for transfers between devices  60.9 us
    all_to_all x1, waiting for transfers between devices, body(): lax.all_to_all(out_weight, 'head', split_axis=1, concat_axis=0, tiled=True)  20 us
    all_gather x1, blocking collectives, body(): all_kv = lax.all_gather(own_kv, 'seq', axis=1, tiled=True)  9.86 us
    all_to_all x1, starting transfers between devices, body(): lax.all_to_all(out_weight, 'head', split_axis=1, concat_axis=0, tiled=True)  6.48 us
    unnamed x25, local copies, waits for them, and re-layouts  5.83 us
    dot_general x1, local copies, waits for them, and re-layouts, body(): jnp.einsum('td,thc->dhc', out_grad, attn, preferred_element_type=jnp.floa...  3.14 us
  transfers between devices with their start and end apart: 2, of which 2 were waited for; matrix products, arithmetic and copies ran while one was open for 2% of the time, Pallas kernels for 0%

commit v1 on v0

--- a/solution.py
+++ b/solution.py
@@ -1,3 +1,4 @@
+import functools
 import math
 import jax
 import jax.numpy as jnp
@@ -7,6 +8,21 @@
 HD = 128
 GROUP = 8
 big_negative = -1e30
+
+
+def save_weights_all(unit, named_axis):
+    return jnp.concatenate(
+        lax.all_to_all(
+            jnp.stack([unit for _ in range(lax.axis_size(named_axis))]),
+            named_axis,
+            split_axis=0,
+            concat_axis=0,
+        ),
+        axis=1,
+    )
+
+
+order_windows_in = functools.partial(save_weights_all, named_axis="seq")
 
 
 def attend_block(query_rows, query_pos, block_kv, key_pos, scale):
@@ -56,7 +72,7 @@
     zeros_col = jnp.zeros((row_total, 1), jnp.float32)
     zeros_rows = jnp.zeros((row_total, HD), jnp.float32)
     lowest_col = jnp.full((row_total, 1), big_negative, jnp.float32)
-    all_kv = lax.all_gather(own_kv, "seq", axis=1, tiled=True)
+    all_kv = order_windows_in(own_kv)
 
     def run_sweep(step_fn, init):
         return sweep(step_fn, init, all_kv, 0, positions)

time: 125 us -> 136 us (1.088)
  waiting for transfers between devices: 80.9 us -> 97.4 us
  blocking collectives: 9.86 us -> 0 us
  starting transfers between devices: 6.48 us -> 10.1 us
    all_gather x1 -> x0, blocking collectives: 9.86 us -> none  [body(): all_kv = lax.all_gather(own_kv, 'seq', axis=1, tiled=True)]
    all_to_all x0 -> x1, waiting for transfers between devices: none -> 8.41 us  [save_weights_all(): lax.all_to_all(jnp.stack([unit for _ in range(lax.axis_size(named_axis))]...]
    all_to_all x1, waiting for transfers between devices: 20 us -> 27.5 us  [body(): lax.all_to_all(out_weight, 'head', split_axis=1, concat_axis=0, tiled=True)]
    all_to_all x0 -> x1, starting transfers between devices: none -> 5.2 us  [save_weights_all(): lax.all_to_all(jnp.stack([unit for _ in range(lax.axis_size(named_axis))]...]
    another operation x0 -> x1, local copies, waits for them, and re-layouts: none -> 1.88 us  [save_weights_all(): jnp.stack([unit for _ in range(lax.axis_size(named_axis))])]
    all_to_all x1, starting transfers between devices: 6.48 us -> 4.87 us  [body(): lax.all_to_all(out_weight, 'head', split_axis=1, concat_axis=0, tiled=True)]
  transfers between devices with their start and end apart: 2 -> 3, of which waited for: 2 -> 3; matrix products, arithmetic and copies ran while one was open for 2% -> 3% of each run, Pallas kernels for 0% -> 0%
where the time goes in v1:
time: 136 us
  waiting for transfers between devices  97.4 us (72%)
  between operations  14.8 us (11%)
  local copies, waits for them, and re-layouts  10.7 us (8%)
  starting transfers between devices  10.1 us (7%)
  matrix products  2.08 us (2%)
    unnamed x2, waiting for transfers between devices  61.5 us
    all_to_all x1, waiting for transfers between devices, body(): lax.all_to_all(out_weight, 'head', split_axis=1, concat_axis=0, tiled=True)  27.5 us
    all_to_all x1, waiting for transfers between devices, save_weights_all(): lax.all_to_all(jnp.stack([unit for _ in range(lax.axis_size(named_axis))]...  8.41 us
    all_to_all x1, starting transfers between devices, save_weights_all(): lax.all_to_all(jnp.stack([unit for _ in range(lax.axis_size(named_axis))]...  5.2 us
    all_to_all x1, starting transfers between devices, body(): lax.all_to_all(out_weight, 'head', split_axis=1, concat_axis=0, tiled=True)  4.87 us
    unnamed x25, local copies, waits for them, and re-layouts  4.52 us
    dot_general x1, local copies, waits for them, and re-layouts, body(): jnp.einsum('td,thc->dhc', out_grad, attn, preferred_element_type=jnp.floa...  3.11 us
  transfers between devices with their start and end apart: 3, of which 3 were waited for; matrix products, arithmetic and copies ran while one was open for 3% of the time, Pallas kernels for 0%

profile of v1, /device:TPU:0, one launch (start us, length us, event | category | flops | bytes accessed | tf_op | source)
XLA Modules:
  0.0 135.8 jit_solution(11906673634596615019)
XLA Ops:
  7.2 1.9 %stack.2 = bf16[8,2,128,128]{3,2,1,0:T(8,128)(2,1)} broadcast(bf16[2,128,128]{2,1,0:T(8,128)(2,1)} %param.6), dimensions={1,2,3} | broadcast | bytes 589824 | tf_op jit(solution)/shard_map/stack | solution.py:16
  9.1 5.2 %all-to-all-start = ((bf16[8,2,128,128]{3,2,1,0:T(8,128)(2,1)}), bf16[8,2,128,128]{3,2,1,0:T(8,128)(2,1)S(1)}, u32[]{:S(2)}, u32[]{:S(2)}) async-start(bf16[8,2,128,128]{3,2,1,0:T(8,128)(2,1)} %stack.2), calls=%async_computation | async-start | bytes 1048576 | tf_op jit(solution)/shard_map/all_to_all | solution.py:15
  14.3 1.3 copy.14
  15.6 8.4 %all-to-all-done = bf16[8,2,128,128]{3,2,1,0:T(8,128)(2,1)S(1)} async-done(((bf16[8,2,128,128]{3,2,1,0:T(8,128)(2,1)}), bf16[8,2,128,128]{3,2,1,0:T(8,128)(2,1)S(1)}, u32[]{:S(2)}, u32[]{:S(2)}) %all-to-all-start) | async-done | bytes 524320 | tf_op jit(solution)/shard_map/all_to_all | solution.py:15
  24.0 4.9 %all-to-all-start.1 = ((bf16[640,8,128]{2,0,1:T(8,128)(2,1)}), bf16[640,8,128]{2,0,1:T(8,128)(2,1)S(1)}, u32[]{:S(2)}, u32[]{:S(2)}) async-start(bf16[640,8,128]{2,0,1:T(8,128)(2,1)} %copy.14), calls=%async_computation.1 | async-start | bytes 2621440 | tf_op jit(solution)/shard_map/all_to_all | solution.py:67
  28.9 0.1 dynamic_slice.16
  29.0 0.1 broadcast_in_dim.38
  29.1 0.1 le.51
  29.3 0.4 fusion.16
  29.7 0.4 fusion.7
  30.1 0.3 fusion.6
  30.4 27.5 %all-to-all-done.1 = bf16[640,8,128]{2,0,1:T(8,128)(2,1)S(1)} async-done(((bf16[640,8,128]{2,0,1:T(8,128)(2,1)}), bf16[640,8,128]{2,0,1:T(8,128)(2,1)S(1)}, u32[]{:S(2)}, u32[]{:S(2)}) %all-to-all-start.1) | async-done | bytes 1310752 | tf_op jit(solution)/shard_map/all_to_all | solution.py:67
  57.9 0.1 copy.15
  58.1 0.4 convolution_convert_fusion
  58.5 0.4 fusion.15
  58.9 0.2 copy-done.6
  59.1 0.5 convolution_bitcast_fusion
  59.7 3.1 %copy.18 = f32[2560,2,128]{2,1,0:T(2,128)} copy(f32[2560,2,128]{0,2,1:T(8,128)S(1)} %convolution_bitcast_fusion) | data formatting | bytes 5242880 | tf_op jit(solution)/shard_map/td,thc->dhc/dot_general | solution.py:115
  62.8 0.6 copy-done.10
  63.4 0.6 dynamic-slice
  64.7 0.4 fusion.5
  65.1 0.7 reshape.48
  65.8 61.5 %all-reduce.3.cloned.1.call-done = f32[2560,2,128]{2,1,0:T(2,128)} async-done(((f32[2560,2,128]{2,1,0:T(2,128)}), f32[2560,2,128]{2,1,0:T(2,128)}) %all-reduce.3.cloned.1.call-update) | async-done | bytes 2621456
  127.3 1.7 %constant_dynamic-slice_fusion = f32[320,2,128]{2,1,0:T(2,128)} fusion(f32[2560,2,128]{2,1,0:T(2,128)} %all-reduce.3.cloned.1.call-done, u32[]{:T(128)S(6)} %multiply.1), kind=kLoop, calls=%fused_computation.21 | loop fusion | bytes 655364
  (27 shorter events, 0.2 us)
Async XLA Ops:
  7.2 50.9 %copy-start = (bf16[128,2560]{1,0:T(8,128)(2,1)S(1)}, bf16[128,2560]{1,0:T(8,128)(2,1)}, u32[]{:S(2)}) copy-start(bf16[128,2560]{1,0:T(8,128)(2,1)} %param.8) | copy-start | bytes 1966084
  7.2 7.1 %copy-start.3 = (bf16[640,8,128]{2,1,0:T(8,128)(2,1)S(1)}, bf16[640,8,128]{2,1,0:T(8,128)(2,1)}, u32[]{:S(2)}) copy-start(bf16[640,8,128]{2,1,0:T(8,128)(2,1)} %param.7) | copy-start | bytes 3932164
  9.1 14.9 %all-to-all-start = ((bf16[8,2,128,128]{3,2,1,0:T(8,128)(2,1)}), bf16[8,2,128,128]{3,2,1,0:T(8,128)(2,1)S(1)}, u32[]{:S(2)}, u32[]{:S(2)}) async-start(bf16[8,2,128,128]{3,2,1,0:T(8,128)(2,1)} %stack.2), calls=%async_computation | async-start | bytes 1048576 | tf_op jit(solution)/shard_map/all_to_all | solution.py:15
  15.6 13.3 %copy-start.8 = (bf16[128,256]{1,0:T(8,128)(2,1)S(1)}, bf16[128,256]{1,0:T(8,128)(2,1)}, u32[]{:S(2)}) copy-start(bf16[128,256]{1,0:T(8,128)(2,1)} %param.5) | copy-start | bytes 196612
  15.6 13.3 %copy-start.9 = (s32[1024]{0:T(1024)S(1)}, s32[1024]{0:T(1024)}, u32[]{:S(2)}) copy-start(s32[1024]{0:T(1024)} %param.9) | copy-start | bytes 12292
  24.0 34.0 %all-to-all-start.1 = ((bf16[640,8,128]{2,0,1:T(8,128)(2,1)}), bf16[640,8,128]{2,0,1:T(8,128)(2,1)S(1)}, u32[]{:S(2)}, u32[]{:S(2)}) async-start(bf16[640,8,128]{2,0,1:T(8,128)(2,1)} %copy.14), calls=%async_computation.1 | async-start | bytes 2621440 | tf_op jit(solution)/shard_map/all_to_all | solution.py:67
  28.9 98.4 %all-reduce.3.cloned.1.call-start = ((), (), s32[]{:S(2)}) async-start(), calls=%async_computation.2 | async-start | bytes 5242880
  29.3 1.1 copy-start.4
  30.4 28.1 %copy-start.1 = (f32[256,1024]{1,0:T(8,128)}, f32[256,1024]{1,0:T(8,128)S(1)}, u32[]{:S(2)}) copy-start(f32[256,1024]{1,0:T(8,128)S(1)} %fusion.6) | copy-start | bytes 3145732
  58.5 0.6 copy-start.6
  62.8 0.7 copy-start.10
  62.8 1.9 %copy-start.2 = (f32[256,1024]{1,0:T(8,128)S(1)}, f32[256,1024]{1,0:T(8,128)}, u32[]{:S(2)}) copy-start(f32[256,1024]{1,0:T(8,128)} %copy-done.1) | copy-start | bytes 3145732
  62.8 1.9 %copy-start.5 = (bf16[1,8,128,128]{3,2,0,1:T(8,128)(2,1)S(1)}, bf16[1,8,128,128]{3,2,0,1:T(8,128)(2,1)}, u32[]{:S(2)}) copy-start(bf16[1,8,128,128]{3,2,0,1:T(8,128)(2,1)} %copy-done.4) | copy-start | bytes 786436
  62.8 1.9 %copy-start.7 = (bf16[128,2,128]{2,1,0:T(2,128)(2,1)S(1)}, bf16[128,2,128]{2,1,0:T(2,128)(2,1)}, u32[]{:S(2)}) copy-start(bf16[128,2,128]{2,1,0:T(2,128)(2,1)} %copy-done.6) | copy-start | bytes 196612
Sparse Core Ops, SparseCore 0:
  62.9 64.2 all-reduce.2
